TPU v7x, 32 devices: a whole 2x2x4 slice. The times are simulated.
32 devices in a mesh: row: 4 (over z), col: 8 (over y, x, core).
Axes of the slice: x: 2, y: 2, z: 4, core: 2. Of those that a mesh axis runs over, the one named last changes fastest.
Arguments:
- rho_real: float32 [4096, 4096], P('row', 'col'), may hold values from -2.5 to 4, as said below
- rho_imag: float32 [4096, 4096], P('row', 'col'), may hold values from -2.5 to 2.5, as said below
- hamiltonian: bfloat16 [4096, 4096], P('row', 'col'), may hold values from -1 to 1
- amplitudes: float32 [8, 4096], replicated, may hold values from 0.15 to 0.6
- offsets: int32 [8], replicated, may hold values from -16 to 16
- active_jumps: int32 [1], replicated, may hold values from 4 to 8
Outputs:
- rho_next_real: float32 [4096, 4096], P('row', 'col')
- rho_next_imag: float32 [4096, 4096], P('row', 'col')
Inputs may be any that keep to these rules, and one draw needn't show every extreme that they name: `rho_real`: symmetric, with every diagonal entry 0.5 or more. `rho_imag`: antisymmetric.
All inputs are finite; a program needn't handle non-finite values.
Results may differ from a plain program's by a relative error of at most 0.001.
Values may be sent and summed in bfloat16 or wider, within the bound.
A program may use at most 192 MiB of HBM per device.

v0:
```python
import jax
import jax.numpy as jnp
from jax import lax
from jax.sharding import PartitionSpec as P

OMAX = 16
step_size = 0.25


def extended(cells, sides, width):
    for axis, dim in sides:
        count = lax.axis_size(axis)
        ends = count - 1
        head = lax.slice_in_dim(cells, 0, width, axis=dim)
        tail = lax.slice_in_dim(cells, cells.shape[dim] - width, cells.shape[dim], axis=dim)
        cells = jnp.concatenate(
            [
                lax.ppermute(tail, axis, [(i, (i + 1) % count) for i in range(ends)]),
                cells,
                lax.ppermute(head, axis, [((i + 1) % count, i) for i in range(ends)]),
            ],
            axis=dim,
        )
    return cells


def dissipate(matrix, padded, amplitudes, offsets, active, row_first, col_first):
    height = matrix.shape[1]
    breadth = matrix.shape[2]
    levels = amplitudes.shape[1]
    margin = (padded.shape[1] - height) // 2
    positions = jnp.arange(levels, dtype=jnp.int32)
    summed = jnp.zeros(matrix.shape, matrix.dtype)
    for jump_slot in range(amplitudes.shape[0]):
        offset = offsets[jump_slot]
        inside = (positions + offset >= 0) & (positions + offset < levels)
        strength = jnp.where(inside, amplitudes[jump_slot], 0.0)
        outflow = jnp.pad(strength * strength, (margin, margin))
        outflow = lax.dynamic_slice_in_dim(outflow, margin - offset, levels)
        row_strength = lax.dynamic_slice_in_dim(strength, row_first, height)
        col_strength = lax.dynamic_slice_in_dim(strength, col_first, breadth)
        row_outflow = lax.dynamic_slice_in_dim(outflow, row_first, height)
        col_outflow = lax.dynamic_slice_in_dim(outflow, col_first, breadth)
        corner = margin + offset
        shifted = lax.dynamic_slice(padded, (jnp.int32(0), corner, corner), (2, height, breadth))
        contribution = (
            row_strength[:, None] * col_strength[None, :] * shifted
            - 0.5 * (row_outflow[:, None] + col_outflow[None, :]) * matrix
        )
        summed = summed + jnp.where(jump_slot < active, contribution, 0.0)
    return summed


def diagonal_sum(matrix, row_first, col_first):
    row_index = lax.broadcasted_iota(jnp.int32, matrix.shape, 0) + row_first
    col_index = lax.broadcasted_iota(jnp.int32, matrix.shape, 1) + col_first
    return jnp.sum(jnp.where(row_index == col_index, matrix, 0.0))


def local(rho_real, rho_imag, hamiltonian, amplitudes, offsets, active_jumps):
    height, breadth = rho_real.shape
    levels = amplitudes.shape[1]
    row_first = lax.axis_index("row") * height
    col_first = lax.axis_index("col") * breadth
    active = active_jumps[0]
    ham_columns = lax.all_gather(hamiltonian, "row", axis=0, tiled=True)
    start_trace = lax.psum(diagonal_sum(rho_real, row_first, col_first), ("row", "col"))

    def drift(real_part, imag_part):
        real_low = real_part.astype(jnp.bfloat16)
        imag_low = imag_part.astype(jnp.bfloat16)
        row_panel = lax.all_gather(hamiltonian, "col", axis=1, tiled=True)
        pieces = (
            lax.all_gather(real_low, "row", axis=0, tiled=True),
            lax.all_gather(imag_low, "row", axis=0, tiled=True),
        )
        strip = row_panel
        left_real = jnp.dot(strip, pieces[0], preferred_element_type=jnp.float32)
        left_imag = jnp.dot(strip, pieces[1], preferred_element_type=jnp.float32)
        pieces = (
            lax.all_gather(real_low, "col", axis=1, tiled=True),
            lax.all_gather(imag_low, "col", axis=1, tiled=True),
        )
        strip = ham_columns
        right_real = jnp.dot(pieces[0], strip, preferred_element_type=jnp.float32)
        right_imag = jnp.dot(pieces[1], strip, preferred_element_type=jnp.float32)
        matrix = jnp.stack([real_part, imag_part])
        padded = extended(matrix.astype(jnp.bfloat16), (("row", 1), ("col", 2)), OMAX).astype(
            matrix.dtype
        )
        loss = dissipate(matrix, padded, amplitudes, offsets, active, row_first, col_first)
        return (left_imag - right_imag + loss[0], right_real - left_real + loss[1])

    first_real, first_imag = drift(rho_real, rho_imag)
    middle_real = rho_real + step_size * first_real
    middle_imag = rho_imag + step_size * first_imag
    rescale = levels / start_trace
    middle_real = middle_real * rescale
    middle_imag = middle_imag * rescale
    second_real, second_imag = drift(middle_real, middle_imag)
    updated_real = rho_real + 0.5 * step_size * (first_real + second_real)
    updated_imag = rho_imag + 0.5 * step_size * (first_imag + second_imag)
    rescale = levels / start_trace
    return (updated_real * rescale, updated_imag * rescale)


def solution(mesh):
    in_specs = (P("row", "col"), P("row", "col"), P("row", "col"), P(), P(), P())
    out_specs = (P("row", "col"), P("row", "col"))
    return jax.shard_map(local, mesh=mesh, in_specs=in_specs, out_specs=out_specs, check_vma=False)
```

profile of v0, /device:TPU:0, one launch (start us, length us, event | category | flops | bytes accessed | tf_op | source)
XLA Modules:
  0.0 739.0 jit_solution(2727342368948847065)
XLA Ops:
  7.2 2.7 convert_element_type.41
  10.0 0.7 all-gather.11.cloned.1.call-update
  12.1 2.0 fusion.1
  14.1 1.3 copy-done.4
  15.4 4.9 collective-permute-start
  20.4 1.3 collective-permute-start.1
  39.6 2.4 add_multiply_fusion.2
  41.9 2.3 add_multiply_fusion.4
  44.3 2.4 add_multiply_fusion.6
  46.7 2.3 add_multiply_fusion.8
  49.0 2.4 broadcast_multiply_fusion
  51.3 2.4 broadcast_multiply_fusion.2
  53.7 2.5 broadcast_multiply_fusion.4
  56.2 1.3 select_reduce_fusion
  58.1 1.5 collective-permute-start.2
  59.8 1.3 collective-permute-start.3
  61.1 2.4 broadcast_multiply_fusion.6
  63.5 47.8 %psum.7 = f32[]{:T(128)} all-reduce(f32[]{:T(128)} %select_reduce_fusion), channel_id=1, replica_groups=mesh['row'=4,'col'=8] {'row','col'}, use_global_device_ids=true, to_apply=%region_1.2 | all-reduce | flops 1 | bytes 8 | tf_op jit(solution)/shard_map/psum | solution.py:67
  128.4 5.1 maximum_convert_fusion
  133.5 28.7 %select_add_fusion.1 = f32[2,1024,512]{2,1,0:T(8,128)} fusion(f32[2,1056,544]{2,1,0:T(8,128)} %maximum_convert_fusion, s32[]{:T(128)S(6)} %select_n.358, s32[]{:T(128)S(6)} %select_n.359, s32[]{:T(128)S(6)} %select_n.351, s32[]{:T(128)S(6)} %select_n.352, s32[]{:T(128)S(6)} %select_n.344, s32[]{:T(128)S(6)} %select_n.345, s32[]{:T(128)S(6)} %select_n.337, ...), kind=kLoop, calls=%fused_computation.3 | loop fusion | flops 41943040 | bytes 75497544 | tf_op jit(solution)/shard_map/add | solution.py:50
  162.2 10.7 %fusion.70 = f32[1024,512]{1,0:T(8,128)} fusion(bf16[1024,4096]{1,0:T(8,128)(2,1)} %all-gather.11.cloned.1.call-done, bf16[4096,512]{1,0:T(8,128)(2,1)} %all-gather.13.cloned.1.call-done), kind=kOutput, calls=%fused_computation.125 | convolution fusion | flops 4294967296 | bytes 14680064 | tf_op jit(solution)/shard_map/dot_general | solution.py:79
  172.9 61.1 %all-gather.17.cloned.1.call-done = bf16[4096,512]{1,0:T(8,128)(2,1)} async-done(((bf16[1024,512]{1,0:T(8,128)(2,1)}), bf16[4096,512]{1,0:T(8,128)(2,1)}) %all-gather.17.cloned.1.call-update) | async-done | bytes 4194320 | tf_op jit(solution)/shard_map/all_gather | solution.py:66
  234.0 56.1 %all-gather.15.cloned.1.call-done = bf16[1024,4096]{1,0:T(8,128)(2,1)} async-done(((bf16[1024,512]{1,0:T(8,128)(2,1)}), bf16[1024,4096]{1,0:T(8,128)(2,1)}) %all-gather.15.cloned.1.call-update) | async-done | bytes 8388624 | tf_op jit(solution)/shard_map/all_gather | solution.py:82
  290.2 10.5 %fusion.13 = f32[1024,512]{1,0:T(8,128)S(1)} fusion(f32[2,1024,512]{2,1,0:T(8,128)} %select_add_fusion.1, f32[1024,512]{1,0:T(8,128)} %fusion.70, bf16[1024,4096]{1,0:T(8,128)(2,1)} %all-gather.15.cloned.1.call-done, bf16[4096,512]{1,0:T(8,128)(2,1)} %all-gather.17.cloned.1.call-done), kind=kOutput, calls=%fused_computation.23 | convolution fusion | flops 4296015872 | bytes 18874368 | tf_op jit(solution)/shard_map/dot_general | solution.py:86
  300.6 2.7 fusion.16
  305.7 53.7 %all-gather.19.cloned.1.call-done = bf16[1024,4096]{1,0:T(8,128)(2,1)} async-done(((bf16[1024,512]{1,0:T(8,128)(2,1)}), bf16[1024,4096]{1,0:T(8,128)(2,1)}) %all-gather.19.cloned.1.call-update) | async-done | bytes 8388624 | tf_op jit(solution)/shard_map/all_gather | solution.py:81
  359.4 10.5 %fusion.71 = f32[1024,512]{1,0:T(8,128)} fusion(bf16[1024,4096]{1,0:T(8,128)(2,1)} %all-gather.19.cloned.1.call-done, bf16[4096,512]{1,0:T(8,128)(2,1)} %all-gather.17.cloned.1.call-done), kind=kOutput, calls=%fused_computation.126 | convolution fusion | flops 4294967296 | bytes 14680064 | tf_op jit(solution)/shard_map/dot_general | solution.py:85
  369.8 71.7 %all-gather.21.cloned.1.call-done = bf16[4096,512]{1,0:T(8,128)(2,1)} async-done(((bf16[1024,512]{1,0:T(8,128)(2,1)}), bf16[4096,512]{1,0:T(8,128)(2,1)}) %all-gather.21.cloned.1.call-update) | async-done | bytes 4194320 | tf_op jit(solution)/shard_map/all_gather | solution.py:74
  441.6 10.3 %fusion.12 = f32[1024,512]{1,0:T(8,128)S(1)} fusion(f32[2,1024,512]{2,1,0:T(8,128)} %select_add_fusion.1, f32[1024,512]{1,0:T(8,128)} %fusion.71, bf16[1024,4096]{1,0:T(8,128)(2,1)} %all-gather.11.cloned.1.call-done, bf16[4096,512]{1,0:T(8,128)(2,1)} %all-gather.21.cloned.1.call-done), kind=kOutput, calls=%fused_computation.21 | convolution fusion | flops 4296015872 | bytes 18874368 | tf_op jit(solution)/shard_map/dot_general | solution.py:78
  451.9 2.5 fusion.15
  454.5 2.6 fusion
  457.1 1.3 copy-done.6
  458.4 1.3 collective-permute-start.4
  459.7 1.3 collective-permute-start.5
  461.3 4.3 collective-permute-done.5
  465.6 1.5 pad_maximum_fusion.4
  467.3 1.3 collective-permute-start.6
  468.8 1.3 collective-permute-start.7
  470.1 27.8 %all-gather.27.cloned.1.call-done = bf16[1024,4096]{1,0:T(8,128)(2,1)} async-done(((bf16[1024,512]{1,0:T(8,128)(2,1)}), bf16[1024,4096]{1,0:T(8,128)(2,1)}) %all-gather.27.cloned.1.call-update) | async-done | bytes 8388624 | tf_op jit(solution)/shard_map/all_gather | solution.py:81
  497.9 10.4 %fusion.73 = f32[1024,512]{1,0:T(8,128)} fusion(bf16[1024,4096]{1,0:T(8,128)(2,1)} %all-gather.27.cloned.1.call-done, bf16[4096,512]{1,0:T(8,128)(2,1)} %all-gather.17.cloned.1.call-done), kind=kOutput, calls=%fused_computation.128 | convolution fusion | flops 4294967296 | bytes 14680064 | tf_op jit(solution)/shard_map/dot_general | solution.py:85
  508.9 5.4 maximum_convert_fusion.1
  514.3 29.5 %select_add_fusion = f32[2,1024,512]{2,1,0:T(8,128)} fusion(f32[2,1056,544]{2,1,0:T(8,128)} %maximum_convert_fusion.1, s32[]{:T(128)S(6)} %select_n.358, s32[]{:T(128)S(6)} %select_n.359, s32[]{:T(128)S(6)} %select_n.351, s32[]{:T(128)S(6)} %select_n.352, s32[]{:T(128)S(6)} %select_n.344, s32[]{:T(128)S(6)} %select_n.345, s32[]{:T(128)S(6)} %select_n.337, ...), kind=kLoop, calls=%fused_computation.2 | loop fusion | flops 41943040 | bytes 75497544 | tf_op jit(solution)/shard_map/add | solution.py:50
  543.7 37.2 %all-gather.29.cloned.1.call-done = bf16[4096,512]{1,0:T(8,128)(2,1)} async-done(((bf16[1024,512]{1,0:T(8,128)(2,1)}), bf16[4096,512]{1,0:T(8,128)(2,1)}) %all-gather.29.cloned.1.call-update) | async-done | bytes 4194320 | tf_op jit(solution)/shard_map/all_gather | solution.py:74
  580.9 12.5 %fusion.6 = f32[1024,512]{1,0:T(8,128)} fusion(f32[1024,512]{1,0:T(8,128)S(1)} %copy-done, f32[1024,512]{1,0:T(8,128)} %copy-done.8, f32[2,1024,512]{2,1,0:T(8,128)} %select_add_fusion, f32[1024,512]{1,0:T(8,128)} %fusion.73, bf16[1024,4096]{1,0:T(8,128)(2,1)} %all-gather.11.cloned.1.call-done, bf16[4096,512]{1,0:T(8,128)(2,1)} %all-gather.29.cloned.1.call-done, ...), kind=kOutput, calls=%fused_computation.13 | convolution fusion | flops 4298113024 | bytes 23068676 | tf_op jit(solution)/shard_map/dot_general | solution.py:78
  593.4 43.8 %all-gather.25.cloned.1.call-done = bf16[1024,4096]{1,0:T(8,128)(2,1)} async-done(((bf16[1024,512]{1,0:T(8,128)(2,1)}), bf16[1024,4096]{1,0:T(8,128)(2,1)}) %all-gather.25.cloned.1.call-update) | async-done | bytes 8388624 | tf_op jit(solution)/shard_map/all_gather | solution.py:82
  637.2 10.5 %fusion.72 = f32[1024,512]{1,0:T(8,128)} fusion(bf16[1024,4096]{1,0:T(8,128)(2,1)} %all-gather.25.cloned.1.call-done, bf16[4096,512]{1,0:T(8,128)(2,1)} %all-gather.17.cloned.1.call-done), kind=kOutput, calls=%fused_computation.127 | convolution fusion | flops 4294967296 | bytes 14680064 | tf_op jit(solution)/shard_map/dot_general | solution.py:86
  647.7 71.7 %all-gather.23.cloned.1.call-done = bf16[4096,512]{1,0:T(8,128)(2,1)} async-done(((bf16[1024,512]{1,0:T(8,128)(2,1)}), bf16[4096,512]{1,0:T(8,128)(2,1)}) %all-gather.23.cloned.1.call-update) | async-done | bytes 4194320 | tf_op jit(solution)/shard_map/all_gather | solution.py:75
  719.4 12.5 %fusion.11 = f32[1024,512]{1,0:T(8,128)} fusion(f32[1024,512]{1,0:T(8,128)S(1)} %copy-done.3, f32[1024,512]{1,0:T(8,128)} %copy-done.7, f32[2,1024,512]{2,1,0:T(8,128)} %select_add_fusion, f32[1024,512]{1,0:T(8,128)} %fusion.72, bf16[1024,4096]{1,0:T(8,128)(2,1)} %all-gather.11.cloned.1.call-done, bf16[4096,512]{1,0:T(8,128)(2,1)} %all-gather.23.cloned.1.call-done, ...), kind=kOutput, calls=%fused_computation.19 | convolution fusion | flops 4298113024 | bytes 23068676 | tf_op jit(solution)/shard_map/dot_general | solution.py:79
  (103 shorter events, 14.1 us)
Async XLA Ops:
  7.2 155.0 %all-gather.13.cloned.1.call-start = ((), (), s32[]{:S(2)}) async-start(), calls=%async_computation.1 | async-start | bytes 5242880 | tf_op jit(solution)/shard_map/all_gather | solution.py:75
  9.9 2.1 copy-start
  10.0 152.2 %all-gather.11.cloned.1.call-start = ((), (), s32[]{:S(2)}) async-start(), calls=%async_computation | async-start | bytes 9437184 | tf_op jit(solution)/shard_map/all_gather | solution.py:72
  10.7 223.3 %all-gather.17.cloned.1.call-start = ((), (), s32[]{:S(2)}) async-start(), calls=%async_computation.3 | async-start | bytes 5242880 | tf_op jit(solution)/shard_map/all_gather | solution.py:66
  11.4 278.7 %all-gather.15.cloned.1.call-start = ((), (), s32[]{:S(2)}) async-start(), calls=%async_computation.2 | async-start | bytes 9437184 | tf_op jit(solution)/shard_map/all_gather | solution.py:82
  12.0 347.3 %all-gather.19.cloned.1.call-start = ((), (), s32[]{:S(2)}) async-start(), calls=%async_computation.4 | async-start | bytes 9437184 | tf_op jit(solution)/shard_map/all_gather | solution.py:81
  12.1 9.6 %copy-start.10 = (s32[8]{0:T(128)S(1)}, s32[8]{0:T(128)}, u32[]{:S(2)}) copy-start(s32[8]{0:T(128)} %param.10) | copy-start | bytes 100
  12.1 20.4 %copy-start.9 = (f32[8,4096]{1,0:T(8,128)S(1)}, f32[8,4096]{1,0:T(8,128)}, u32[]{:S(2)}) copy-start(f32[8,4096]{1,0:T(8,128)} %param.9) | copy-start | bytes 393220
  14.1 1.3 copy-start.4
  15.4 42.2 %collective-permute-start = (bf16[2,16,512]{2,1,0:T(8,128)(2,1)S(1)}, bf16[2,16,512]{2,1,0:T(8,128)(2,1)S(1)}, u32[]{:S(2)}, u32[]{:S(2)}) collective-permute-start(bf16[2,16,512]{2,1,0:T(8,128)(2,1)S(1)} %get-tuple-element.29), channel_id=1, source_target_pairs={{0,8},{8,16},{16,24},{1,9},{9,17},{17,25},{2,10},{10,18},{18,26},{... | collective-permute-start | bytes 98312 | tf_op jit(solution)/shard_map/ppermute | solution.py:18
  20.4 37.3 %collective-permute-start.1 = (bf16[2,16,512]{2,1,0:T(8,128)(2,1)S(1)}, bf16[2,16,512]{2,1,0:T(8,128)(2,1)S(1)}, u32[]{:S(2)}, u32[]{:S(2)}) collective-permute-start(bf16[2,16,512]{2,1,0:T(8,128)(2,1)S(1)} %get-tuple-element.30), channel_id=1, source_target_pairs={{8,0},{16,8},{24,16},{9,1},{17,9},{25,17},{10,2},{18,10},{26,18},{... | collective-permute-start | bytes 98312 | tf_op jit(solution)/shard_map/ppermute | solution.py:20
  53.7 2.5 copy-start.1
  53.7 3.9 copy-start.5
  58.1 69.7 %collective-permute-start.2 = (bf16[2,1056,16]{1,2,0:T(8,128)(2,1)S(1)}, bf16[2,1056,16]{1,2,0:T(8,128)(2,1)S(1)}, u32[]{:S(2)}, u32[]{:S(2)}) collective-permute-start(bf16[2,1056,16]{1,2,0:T(8,128)(2,1)S(1)} %copy.10), channel_id=1, source_target_pairs={{0,1},{1,2},{2,3},{3,4},{4,5},{5,6},{6,7},{8,9},{9,10},{10,11},{11... | collective-permute-start | bytes 202760 | tf_op jit(solution)/shard_map/ppermute | solution.py:18
  59.8 68.3 %collective-permute-start.3 = (bf16[2,1056,16]{1,2,0:T(8,128)(2,1)S(1)}, bf16[2,1056,16]{1,2,0:T(8,128)(2,1)S(1)}, u32[]{:S(2)}, u32[]{:S(2)}) collective-permute-start(bf16[2,1056,16]{1,2,0:T(8,128)(2,1)S(1)} %copy.11), channel_id=1, source_target_pairs={{1,0},{2,1},{3,2},{4,3},{5,4},{6,5},{7,6},{9,8},{10,9},{11,10},{12... | collective-permute-start | bytes 202760 | tf_op jit(solution)/shard_map/ppermute | solution.py:20
  290.1 10.5 %copy-start.2 = (f32[1024,512]{1,0:T(8,128)S(1)}, f32[1024,512]{1,0:T(8,128)}, u32[]{:S(2)}) copy-start(f32[1024,512]{1,0:T(8,128)} %param.6) | copy-start | bytes 6291460
  300.6 2.7 copy-start.7
  303.4 138.2 %all-gather.21.cloned.1.call-start = ((), (), s32[]{:S(2)}) async-start(), calls=%async_computation.5 | async-start | bytes 5242880 | tf_op jit(solution)/shard_map/all_gather | solution.py:74
  303.9 194.0 %all-gather.27.cloned.1.call-start = ((), (), s32[]{:S(2)}) async-start(), calls=%async_computation.8 | async-start | bytes 9437184 | tf_op jit(solution)/shard_map/all_gather | solution.py:81
  304.7 276.3 %all-gather.29.cloned.1.call-start = ((), (), s32[]{:S(2)}) async-start(), calls=%async_computation.9 | async-start | bytes 5242880 | tf_op jit(solution)/shard_map/all_gather | solution.py:74
  305.4 331.8 %all-gather.25.cloned.1.call-start = ((), (), s32[]{:S(2)}) async-start(), calls=%async_computation.7 | async-start | bytes 9437184 | tf_op jit(solution)/shard_map/all_gather | solution.py:82
  451.9 2.5 copy-start.8
  454.4 265.0 %all-gather.23.cloned.1.call-start = ((), (), s32[]{:S(2)}) async-start(), calls=%async_computation.6 | async-start | bytes 5242880 | tf_op jit(solution)/shard_map/all_gather | solution.py:75
  457.1 1.3 copy-start.6
  458.4 2.9 collective-permute-start.4
  459.7 5.9 collective-permute-start.5
  467.3 41.0 %collective-permute-start.6 = (bf16[2,1056,16]{1,2,0:T(8,128)(2,1)S(1)}, bf16[2,1056,16]{1,2,0:T(8,128)(2,1)S(1)}, u32[]{:S(2)}, u32[]{:S(2)}) collective-permute-start(bf16[2,1056,16]{1,2,0:T(8,128)(2,1)S(1)} %copy.15), channel_id=1, source_target_pairs={{0,1},{1,2},{2,3},{3,4},{4,5},{5,6},{6,7},{8,9},{9,10},{10,11},{11... | collective-permute-start | bytes 202760 | tf_op jit(solution)/shard_map/ppermute | solution.py:18
  468.8 39.8 %collective-permute-start.7 = (bf16[2,1056,16]{1,2,0:T(8,128)(2,1)S(1)}, bf16[2,1056,16]{1,2,0:T(8,128)(2,1)S(1)}, u32[]{:S(2)}, u32[]{:S(2)}) collective-permute-start(bf16[2,1056,16]{1,2,0:T(8,128)(2,1)S(1)} %copy.16), channel_id=1, source_target_pairs={{1,0},{2,1},{3,2},{4,3},{5,4},{6,5},{7,6},{9,8},{10,9},{11,10},{12... | collective-permute-start | bytes 202760 | tf_op jit(solution)/shard_map/ppermute | solution.py:20
  593.4 126.0 %copy-start.3 = (f32[1024,512]{1,0:T(8,128)S(1)}, f32[1024,512]{1,0:T(8,128)}, u32[]{:S(2)}) copy-start(f32[1024,512]{1,0:T(8,128)} %param.6) | copy-start | bytes 6291460
Sparse Core Ops, SparseCore 0:
  10.1 84.7 all-gather.12
  96.7 54.9 all-gather.10
  153.3 80.7 all-gather.16
  235.8 54.3 all-gather.14
  303.5 55.8 all-gather.18
  360.8 80.7 all-gather.20
  443.4 54.4 all-gather.26
  499.5 81.4 all-gather.28
  582.8 54.3 all-gather.24
  638.6 80.7 all-gather.22
where the time goes:
time: 744 us; the launch traced here: 739 us
  waiting for transfers between devices  432 us (58%)
  other arithmetic  108 us (15%)
  matrix products  87.7 us (12%)
  blocking collectives  47.8 us (6%)
  between operations  41.4 us (6%)
  starting transfers between devices  14.7 us (2%)
    all_gather x2, waiting for transfers between devices, drift(): lax.all_gather(real_low, 'row', axis=0, tiled=True)  109 us
    all_gather x2, waiting for transfers between devices, drift(): lax.all_gather(imag_low, 'col', axis=1, tiled=True)  99.9 us
    all_gather x2, waiting for transfers between devices, drift(): lax.all_gather(real_low, 'col', axis=1, tiled=True)  81.5 us
    all_gather x2, waiting for transfers between devices, drift(): lax.all_gather(imag_low, 'row', axis=0, tiled=True)  71.7 us
    all_gather x1, waiting for transfers between devices, local(): ham_columns = lax.all_gather(hamiltonian, 'row', axis=0, tiled=True)  61.1 us
    add x2, other arithmetic, dissipate(): summed = summed + jnp.where(jump_slot < active, contribution, 0.0)  58.1 us
    psum x1, blocking collectives, local(): lax.psum(diagonal_sum(rho_real, row_first, col_first), ('row', 'col'))  47.8 us
    dot_general x2, matrix products, drift(): left_imag = jnp.dot(strip, pieces[1], preferred_element_type=jnp.float32)  23.2 us
  transfers between devices with their start and end apart: 18, of which 10 were waited for; matrix products, arithmetic and copies ran while one was open for 23% of the time, Pallas kernels for 0%

commit v1 on v0

--- a/solution.py
+++ b/solution.py
@@ -63,7 +63,12 @@
     row_first = lax.axis_index("row") * height
     col_first = lax.axis_index("col") * breadth
     active = active_jumps[0]
-    ham_columns = lax.all_gather(hamiltonian, "row", axis=0, tiled=True)
+    ring = [hamiltonian]
+    for hop in range(3):
+        ring.append(lax.ppermute(ring[-1], "row", [(dev, (dev + 1) % 4) for dev in range(4)]))
+    ham_columns = jnp.roll(
+        jnp.concatenate(ring[::-1], axis=0), (lax.axis_index("row") + 1) * ring[0].shape[0], axis=0
+    )
     start_trace = lax.psum(diagonal_sum(rho_real, row_first, col_first), ("row", "col"))
 
     def drift(real_part, imag_part):

time: 744 us -> 701 us (0.942)
  waiting for transfers between devices: 432 us -> 326 us
  blocking collectives: 47.8 us -> 70.9 us
  local copies, waits for them, and re-layouts: 7.37 us -> 27 us
  starting transfers between devices: 14.7 us -> 33.5 us
    all_gather x1 -> x0, waiting for transfers between devices: 61.1 us -> none  [local(): ham_columns = lax.all_gather(hamiltonian, 'row', axis=0, tiled=True)]
    all_gather x2, waiting for transfers between devices: 99.9 us -> 60.6 us  [drift(): lax.all_gather(imag_low, 'col', axis=1, tiled=True)]
    all_gather x2, waiting for transfers between devices: 81.5 us -> 55.8 us  [drift(): lax.all_gather(real_low, 'col', axis=1, tiled=True)]
    psum x1, blocking collectives: 47.8 us -> 70.9 us  [local(): lax.psum(diagonal_sum(rho_real, row_first, col_first), ('row', 'col'))]
    all_gather x2, waiting for transfers between devices: 109 us -> 130 us  [drift(): lax.all_gather(real_low, 'row', axis=0, tiled=True)]
    ppermute x0 -> x3, starting transfers between devices: none -> 17.7 us  [local(): lax.ppermute(ring[-1], 'row', [(dev, (dev + 1) % 4) for dev in range(4)])]
    unnamed x22 -> x31, local copies, waits for them, and re-layouts: 2.66 us -> 17.7 us
  transfers between devices with their start and end apart: 18 -> 20, of which waited for: 10 -> 9; matrix products, arithmetic and copies ran while one was open for 23% -> 28% of each run, Pallas kernels for 0% -> 0%
where the time goes in v1:
time: 701 us; the launch traced here: 693 us
  waiting for transfers between devices  326 us (47%)
  other arithmetic  108 us (15%)
  matrix products  87.7 us (13%)
  blocking collectives  70.9 us (10%)
  between operations  40.1 us (6%)
  starting transfers between devices  33.5 us (5%)
  local copies, waits for them, and re-layouts  27 us (4%)
    all_gather x2, waiting for transfers between devices, drift(): lax.all_gather(real_low, 'row', axis=0, tiled=True)  130 us
    psum x1, blocking collectives, local(): lax.psum(diagonal_sum(rho_real, row_first, col_first), ('row', 'col'))  70.9 us
    all_gather x2, waiting for transfers between devices, drift(): lax.all_gather(imag_low, 'row', axis=0, tiled=True)  69.9 us
    all_gather x2, waiting for transfers between devices, drift(): lax.all_gather(imag_low, 'col', axis=1, tiled=True)  60.6 us
    add x2, other arithmetic, dissipate(): summed = summed + jnp.where(jump_slot < active, contribution, 0.0)  59 us
    all_gather x2, waiting for transfers between devices, drift(): lax.all_gather(real_low, 'col', axis=1, tiled=True)  55.8 us
    dot_general x2, matrix products, drift(): right_imag = jnp.dot(pieces[1], strip, preferred_element_type=jnp.float32)  22.9 us
    dot_general x2, matrix products, drift(): right_real = jnp.dot(pieces[0], strip, preferred_element_type=jnp.float32)  22.8 us
  transfers between devices with their start and end apart: 20, of which 9 were waited for; matrix products, arithmetic and copies ran while one was open for 28% of the time, Pallas kernels for 0%

profile of v1, /device:TPU:0, one launch (start us, length us, event | category | flops | bytes accessed | tf_op | source)
XLA Modules:
  0.0 693.2 jit_solution(11660752191076876711)
XLA Ops:
  7.2 2.9 convert_element_type.41
  11.7 3.1 collective-permute-start
  14.8 1.9 fusion.1
  16.8 1.3 copy-done.4
  18.1 3.5 collective-permute-start.3
  40.3 2.4 add_multiply_fusion.2
  42.6 2.3 add_multiply_fusion.4
  44.9 2.4 add_multiply_fusion.6
  47.3 2.3 add_multiply_fusion.8
  49.6 2.4 broadcast_multiply_fusion
  52.0 2.3 broadcast_multiply_fusion.2
  54.3 2.3 broadcast_multiply_fusion.4
  58.1 14.2 %collective-permute-start.1 = (bf16[1024,512]{1,0:T(8,128)(2,1)}, bf16[1024,512]{1,0:T(8,128)(2,1)}, u32[]{:S(2)}, u32[]{:S(2)}) collective-permute-start(bf16[1024,512]{1,0:T(8,128)(2,1)} %collective-permute-done), channel_id=1, source_target_pairs={{0,8},{8,16},{16,24},{24,0},{1,9},{9,17},{17,25},{25,1},{2,10},{10... | collective-permute-start | bytes 3145736 | tf_op jit(solution)/shard_map/ppermute | solution.py:68
  74.7 1.3 collective-permute-start.5
  78.6 2.3 broadcast_multiply_fusion.6
  80.9 70.9 %psum.7 = f32[]{:T(128)} all-reduce(f32[]{:T(128)} %select_reduce_fusion), channel_id=1, replica_groups=mesh['row'=4,'col'=8] {'row','col'}, use_global_device_ids=true, to_apply=%region_1.2 | all-reduce | flops 1 | bytes 8 | tf_op jit(solution)/shard_map/psum | solution.py:72
  169.7 5.2 maximum_convert_fusion
  175.4 29.2 %select_add_fusion.1 = f32[2,1024,512]{2,1,0:T(8,128)} fusion(f32[2,1056,544]{2,1,0:T(8,128)} %maximum_convert_fusion, s32[]{:T(128)S(6)} %select_n.373, s32[]{:T(128)S(6)} %select_n.374, s32[]{:T(128)S(6)} %select_n.366, s32[]{:T(128)S(6)} %select_n.367, s32[]{:T(128)S(6)} %select_n.359, s32[]{:T(128)S(6)} %select_n.360, s32[]{:T(128)S(6)} %select_n.352, ...), kind=kLoop, calls=%fused_computation.3 | loop fusion | flops 41943040 | bytes 75497544 | tf_op jit(solution)/shard_map/add | solution.py:50
  204.6 2.2 constant_dynamic-update-slice_fusion.7
  206.9 2.3 constant_dynamic-update-slice_fusion.6
  209.1 2.3 constant_dynamic-update-slice_fusion.5
  212.5 2.3 constant_dynamic-update-slice_fusion.3
  214.8 2.3 constant_dynamic-update-slice_fusion.2
  217.0 2.6 constant_dynamic-update-slice_fusion.1
  220.7 10.6 %fusion.90 = f32[1024,512]{1,0:T(8,128)} fusion(bf16[1024,4096]{1,0:T(8,128)(2,1)} %all-gather.10.cloned.1.call-done, bf16[4096,512]{1,0:T(8,128)(2,1)} %all-gather.12.cloned.1.call-done), kind=kOutput, calls=%fused_computation.147 | convolution fusion | flops 4294967296 | bytes 14680064 | tf_op jit(solution)/shard_map/dot_general | solution.py:84
  231.3 14.7 %all-gather.14.cloned.1.call-done = bf16[1024,4096]{1,0:T(8,128)(2,1)} async-done(((bf16[1024,512]{1,0:T(8,128)(2,1)}), bf16[1024,4096]{1,0:T(8,128)(2,1)}) %all-gather.14.cloned.1.call-update) | async-done | bytes 8388624 | tf_op jit(solution)/shard_map/all_gather | solution.py:87
  246.0 10.5 %fusion.21 = f32[1024,512]{1,0:T(8,128)S(1)} fusion(f32[2,1024,512]{2,1,0:T(8,128)} %select_add_fusion.1, f32[1024,512]{1,0:T(8,128)} %fusion.90, bf16[1024,4096]{1,0:T(8,128)(2,1)} %all-gather.14.cloned.1.call-done, bf16[8192,512]{1,0:T(8,128)(2,1)} %constant_dynamic-update-slice_fusion, s32[]{:T(128)S(6)} %select_n.317), kind=kOutput, calls=%fused_computation.31 | convolution fusion | flops 4296015872 | bytes 18874372 | tf_op jit(solution)/shard_map/dot_general | solution.py:91
  256.5 2.7 fusion.32
  261.4 78.8 %all-gather.18.cloned.1.call-done = bf16[4096,512]{1,0:T(8,128)(2,1)} async-done(((bf16[1024,512]{1,0:T(8,128)(2,1)}), bf16[4096,512]{1,0:T(8,128)(2,1)}) %all-gather.18.cloned.1.call-update) | async-done | bytes 4194320 | tf_op jit(solution)/shard_map/all_gather | solution.py:79
  340.1 10.3 %fusion.91 = f32[1024,512]{1,0:T(8,128)} fusion(bf16[1024,4096]{1,0:T(8,128)(2,1)} %all-gather.10.cloned.1.call-done, bf16[4096,512]{1,0:T(8,128)(2,1)} %all-gather.18.cloned.1.call-done), kind=kOutput, calls=%fused_computation.148 | convolution fusion | flops 4294967296 | bytes 14680064 | tf_op jit(solution)/shard_map/dot_general | solution.py:83
  350.5 45.8 %all-gather.16.cloned.1.call-done = bf16[1024,4096]{1,0:T(8,128)(2,1)} async-done(((bf16[1024,512]{1,0:T(8,128)(2,1)}), bf16[1024,4096]{1,0:T(8,128)(2,1)}) %all-gather.16.cloned.1.call-update) | async-done | bytes 8388624 | tf_op jit(solution)/shard_map/all_gather | solution.py:86
  396.2 10.3 %fusion.20 = f32[1024,512]{1,0:T(8,128)S(1)} fusion(f32[2,1024,512]{2,1,0:T(8,128)} %select_add_fusion.1, f32[1024,512]{1,0:T(8,128)} %fusion.91, bf16[1024,4096]{1,0:T(8,128)(2,1)} %all-gather.16.cloned.1.call-done, bf16[8192,512]{1,0:T(8,128)(2,1)} %constant_dynamic-update-slice_fusion, s32[]{:T(128)S(6)} %select_n.317), kind=kOutput, calls=%fused_computation.29 | convolution fusion | flops 4296015872 | bytes 18874372 | tf_op jit(solution)/shard_map/dot_general | solution.py:90
  407.9 2.2 fusion.31
  410.8 2.6 fusion
  413.4 3.4 collective-permute-start.7
  419.1 4.6 collective-permute-done.8
  424.2 1.9 collective-permute-start.9
  426.3 1.3 collective-permute-start.10
  427.6 51.5 %all-gather.26.cloned.1.call-done = bf16[4096,512]{1,0:T(8,128)(2,1)} async-done(((bf16[1024,512]{1,0:T(8,128)(2,1)}), bf16[4096,512]{1,0:T(8,128)(2,1)}) %all-gather.26.cloned.1.call-update) | async-done | bytes 4194320 | tf_op jit(solution)/shard_map/all_gather | solution.py:79
  479.1 10.6 %fusion.93 = f32[512,1024]{0,1:T(8,128)} fusion(bf16[1024,4096]{1,0:T(8,128)(2,1)} %all-gather.10.cloned.1.call-done, bf16[4096,512]{1,0:T(8,128)(2,1)} %all-gather.26.cloned.1.call-done), kind=kOutput, calls=%fused_computation.150 | convolution fusion | flops 4294967296 | bytes 14680064 | tf_op jit(solution)/shard_map/dot_general | solution.py:83
  490.3 5.3 maximum_convert_fusion.1
  495.6 29.7 %select_add_fusion = f32[2,1024,512]{2,1,0:T(8,128)} fusion(f32[2,1056,544]{2,1,0:T(8,128)} %maximum_convert_fusion.1, s32[]{:T(128)S(6)} %select_n.373, s32[]{:T(128)S(6)} %select_n.374, s32[]{:T(128)S(6)} %select_n.366, s32[]{:T(128)S(6)} %select_n.367, s32[]{:T(128)S(6)} %select_n.359, s32[]{:T(128)S(6)} %select_n.360, s32[]{:T(128)S(6)} %select_n.352, ...), kind=kLoop, calls=%fused_computation.2 | loop fusion | flops 41943040 | bytes 75497544 | tf_op jit(solution)/shard_map/add | solution.py:50
  525.3 10.1 %all-gather.24.cloned.1.call-done = bf16[1024,4096]{1,0:T(8,128)(2,1)} async-done(((bf16[1024,512]{1,0:T(8,128)(2,1)}), bf16[1024,4096]{1,0:T(8,128)(2,1)}) %all-gather.24.cloned.1.call-update) | async-done | bytes 8388624 | tf_op jit(solution)/shard_map/all_gather | solution.py:86
  535.4 12.5 %fusion.14 = f32[1024,512]{1,0:T(8,128)} fusion(f32[1024,512]{1,0:T(8,128)S(1)} %copy-done, f32[1024,512]{1,0:T(8,128)} %copy-done.9, f32[2,1024,512]{2,1,0:T(8,128)} %select_add_fusion, f32[512,1024]{0,1:T(8,128)} %fusion.93, bf16[1024,4096]{1,0:T(8,128)(2,1)} %all-gather.24.cloned.1.call-done, bf16[8192,512]{1,0:T(8,128)(2,1)} %constant_dynamic-update-slice_fusion, ...), kind=kOutput, calls=%fused_computation.21 | convolution fusion | flops 4298113024 | bytes 23068680 | tf_op jit(solution)/shard_map/dot_general | solution.py:90
  547.8 69.9 %all-gather.20.cloned.1.call-done = bf16[4096,512]{1,0:T(8,128)(2,1)} async-done(((bf16[1024,512]{1,0:T(8,128)(2,1)}), bf16[4096,512]{1,0:T(8,128)(2,1)}) %all-gather.20.cloned.1.call-update) | async-done | bytes 4194320 | tf_op jit(solution)/shard_map/all_gather | solution.py:80
  617.7 10.4 %fusion.92 = f32[512,1024]{0,1:T(8,128)} fusion(bf16[1024,4096]{1,0:T(8,128)(2,1)} %all-gather.10.cloned.1.call-done, bf16[4096,512]{1,0:T(8,128)(2,1)} %all-gather.20.cloned.1.call-done), kind=kOutput, calls=%fused_computation.149 | convolution fusion | flops 4294967296 | bytes 14680064 | tf_op jit(solution)/shard_map/dot_general | solution.py:84
  628.1 45.9 %all-gather.22.cloned.1.call-done = bf16[1024,4096]{1,0:T(8,128)(2,1)} async-done(((bf16[1024,512]{1,0:T(8,128)(2,1)}), bf16[1024,4096]{1,0:T(8,128)(2,1)}) %all-gather.22.cloned.1.call-update) | async-done | bytes 8388624 | tf_op jit(solution)/shard_map/all_gather | solution.py:87
  674.0 12.5 %fusion.19 = f32[1024,512]{1,0:T(8,128)} fusion(f32[1024,512]{1,0:T(8,128)S(1)} %copy-done.3, f32[1024,512]{1,0:T(8,128)} %copy-done.8, f32[2,1024,512]{2,1,0:T(8,128)} %select_add_fusion, f32[512,1024]{0,1:T(8,128)} %fusion.92, bf16[1024,4096]{1,0:T(8,128)(2,1)} %all-gather.22.cloned.1.call-done, bf16[8192,512]{1,0:T(8,128)(2,1)} %constant_dynamic-update-slice_fusion, ...), kind=kOutput, calls=%fused_computation.27 | convolution fusion | flops 4298113024 | bytes 23068680 | tf_op jit(solution)/shard_map/dot_general | solution.py:91
  (116 shorter events, 29.0 us)
Async XLA Ops:
  7.2 7.7 %copy-start = (f32[1024,512]{1,0:T(8,128)S(1)}, f32[1024,512]{1,0:T(8,128)}, u32[]{:S(2)}) copy-start(f32[1024,512]{1,0:T(8,128)} %param.7) | copy-start | bytes 6291460
  7.2 4.6 copy-start.7
  7.2 213.5 %all-gather.12.cloned.1.call-start = ((), (), s32[]{:S(2)}) async-start(), calls=%async_computation.1 | async-start | bytes 5242880 | tf_op jit(solution)/shard_map/all_gather | solution.py:80
  10.2 12.7 %copy-start.11 = (s32[8]{0:T(128)S(1)}, s32[8]{0:T(128)}, u32[]{:S(2)}) copy-start(s32[8]{0:T(128)} %param.10) | copy-start | bytes 100
  10.2 23.2 %copy-start.10 = (f32[8,4096]{1,0:T(8,128)S(1)}, f32[8,4096]{1,0:T(8,128)}, u32[]{:S(2)}) copy-start(f32[8,4096]{1,0:T(8,128)} %param.9) | copy-start | bytes 393220
  10.2 210.5 %all-gather.10.cloned.1.call-start = ((), (), s32[]{:S(2)}) async-start(), calls=%async_computation | async-start | bytes 9437184 | tf_op jit(solution)/shard_map/all_gather | solution.py:77
  10.9 235.0 %all-gather.14.cloned.1.call-start = ((), (), s32[]{:S(2)}) async-start(), calls=%async_computation.2 | async-start | bytes 9437184 | tf_op jit(solution)/shard_map/all_gather | solution.py:87
  11.7 328.5 %all-gather.18.cloned.1.call-start = ((), (), s32[]{:S(2)}) async-start(), calls=%async_computation.4 | async-start | bytes 5242880 | tf_op jit(solution)/shard_map/all_gather | solution.py:79
  11.7 46.3 %collective-permute-start = (bf16[1024,512]{1,0:T(8,128)(2,1)S(1)}, bf16[1024,512]{1,0:T(8,128)(2,1)}, u32[]{:S(2)}, u32[]{:S(2)}) collective-permute-start(bf16[1024,512]{1,0:T(8,128)(2,1)S(1)} %copy-done.7), channel_id=1, source_target_pairs={{0,8},{8,16},{16,24},{24,0},{1,9},{9,17},{17,25},{25,1},{2,10},{10... | collective-permute-start | bytes 3145736 | tf_op jit(solution)/shard_map/ppermute | solution.py:68
  16.8 1.3 copy-start.4
  18.1 54.1 %collective-permute-start.3 = (bf16[2,16,512]{2,1,0:T(8,128)(2,1)S(1)}, bf16[2,16,512]{2,1,0:T(8,128)(2,1)S(1)}, u32[]{:S(2)}, u32[]{:S(2)}) collective-permute-start(bf16[2,16,512]{2,1,0:T(8,128)(2,1)S(1)} %get-tuple-element.29), channel_id=1, source_target_pairs={{0,8},{8,16},{16,24},{1,9},{9,17},{17,25},{2,10},{10,18},{18,26},{... | collective-permute-start | bytes 98312 | tf_op jit(solution)/shard_map/ppermute | solution.py:18
  21.6 50.6 %collective-permute-start.4 = (bf16[2,16,512]{2,1,0:T(8,128)(2,1)S(1)}, bf16[2,16,512]{2,1,0:T(8,128)(2,1)S(1)}, u32[]{:S(2)}, u32[]{:S(2)}) collective-permute-start(bf16[2,16,512]{2,1,0:T(8,128)(2,1)S(1)} %get-tuple-element.30), channel_id=1, source_target_pairs={{8,0},{16,8},{24,16},{9,1},{17,9},{25,17},{10,2},{18,10},{26,18},{... | collective-permute-start | bytes 98312 | tf_op jit(solution)/shard_map/ppermute | solution.py:20
  52.0 4.7 copy-start.1
  54.3 17.9 %copy-start.5 = (bf16[2,1024,512]{2,1,0:T(8,128)(2,1)S(1)}, bf16[2,1024,512]{2,1,0:T(8,128)(2,1)}, u32[]{:S(2)}) copy-start(bf16[2,1024,512]{2,1,0:T(8,128)(2,1)} %copy-done.4) | copy-start | bytes 6291460
  58.1 116.8 %collective-permute-start.1 = (bf16[1024,512]{1,0:T(8,128)(2,1)}, bf16[1024,512]{1,0:T(8,128)(2,1)}, u32[]{:S(2)}, u32[]{:S(2)}) collective-permute-start(bf16[1024,512]{1,0:T(8,128)(2,1)} %collective-permute-done), channel_id=1, source_target_pairs={{0,8},{8,16},{16,24},{24,0},{1,9},{9,17},{17,25},{25,1},{2,10},{10... | collective-permute-start | bytes 3145736 | tf_op jit(solution)/shard_map/ppermute | solution.py:68
  74.7 92.9 %collective-permute-start.5 = (bf16[2,1056,16]{1,2,0:T(8,128)(2,1)S(1)}, bf16[2,1056,16]{1,2,0:T(8,128)(2,1)S(1)}, u32[]{:S(2)}, u32[]{:S(2)}) collective-permute-start(bf16[2,1056,16]{1,2,0:T(8,128)(2,1)S(1)} %copy.13), channel_id=1, source_target_pairs={{0,1},{1,2},{2,3},{3,4},{4,5},{5,6},{6,7},{8,9},{9,10},{10,11},{11... | collective-permute-start | bytes 202760 | tf_op jit(solution)/shard_map/ppermute | solution.py:18
  77.3 91.4 %collective-permute-start.6 = (bf16[2,1056,16]{1,2,0:T(8,128)(2,1)S(1)}, bf16[2,1056,16]{1,2,0:T(8,128)(2,1)S(1)}, u32[]{:S(2)}, u32[]{:S(2)}) collective-permute-start(bf16[2,1056,16]{1,2,0:T(8,128)(2,1)S(1)} %copy.14), channel_id=1, source_target_pairs={{1,0},{2,1},{3,2},{4,3},{5,4},{6,5},{7,6},{9,8},{10,9},{11,10},{12... | collective-permute-start | bytes 202760 | tf_op jit(solution)/shard_map/ppermute | solution.py:20
  174.9 29.7 %collective-permute-start.2 = (bf16[1024,512]{1,0:T(8,128)(2,1)}, bf16[1024,512]{1,0:T(8,128)(2,1)}, u32[]{:S(2)}, u32[]{:S(2)}) collective-permute-start(bf16[1024,512]{1,0:T(8,128)(2,1)} %collective-permute-done.1), channel_id=1, source_target_pairs={{0,8},{8,16},{16,24},{24,0},{1,9},{9,17},{17,25},{25,1},{2,10},{10... | collective-permute-start | bytes 3145736 | tf_op jit(solution)/shard_map/ppermute | solution.py:68
  246.0 10.5 %copy-start.2 = (f32[1024,512]{1,0:T(8,128)S(1)}, f32[1024,512]{1,0:T(8,128)}, u32[]{:S(2)}) copy-start(f32[1024,512]{1,0:T(8,128)} %param.6) | copy-start | bytes 6291460
  256.5 2.8 copy-start.8
  259.2 137.0 %all-gather.16.cloned.1.call-start = ((), (), s32[]{:S(2)}) async-start(), calls=%async_computation.3 | async-start | bytes 9437184 | tf_op jit(solution)/shard_map/all_gather | solution.py:86
  259.8 219.3 %all-gather.26.cloned.1.call-start = ((), (), s32[]{:S(2)}) async-start(), calls=%async_computation.8 | async-start | bytes 5242880 | tf_op jit(solution)/shard_map/all_gather | solution.py:79
  260.4 274.9 %all-gather.24.cloned.1.call-start = ((), (), s32[]{:S(2)}) async-start(), calls=%async_computation.7 | async-start | bytes 9437184 | tf_op jit(solution)/shard_map/all_gather | solution.py:86
  261.2 356.5 %all-gather.20.cloned.1.call-start = ((), (), s32[]{:S(2)}) async-start(), calls=%async_computation.5 | async-start | bytes 5242880 | tf_op jit(solution)/shard_map/all_gather | solution.py:80
  406.6 1.3 copy-start.9
  410.1 263.9 %all-gather.22.cloned.1.call-start = ((), (), s32[]{:S(2)}) async-start(), calls=%async_computation.6 | async-start | bytes 9437184 | tf_op jit(solution)/shard_map/all_gather | solution.py:87
  413.4 10.3 %copy-start.6 = (bf16[2,1024,512]{2,1,0:T(8,128)(2,1)}, bf16[2,1024,512]{2,1,0:T(8,128)(2,1)S(1)}, u32[]{:S(2)}) copy-start(bf16[2,1024,512]{2,1,0:T(8,128)(2,1)S(1)} %fusion) | copy-start | bytes 6291460
  413.4 5.7 collective-permute-start.7
  416.8 6.9 collective-permute-start.8
  424.2 65.5 %collective-permute-start.9 = (bf16[2,1056,16]{1,2,0:T(8,128)(2,1)S(1)}, bf16[2,1056,16]{1,2,0:T(8,128)(2,1)S(1)}, u32[]{:S(2)}, u32[]{:S(2)}) collective-permute-start(bf16[2,1056,16]{1,2,0:T(8,128)(2,1)S(1)} %copy.19), channel_id=1, source_target_pairs={{0,1},{1,2},{2,3},{3,4},{4,5},{5,6},{6,7},{8,9},{9,10},{10,11},{11... | collective-permute-start | bytes 202760 | tf_op jit(solution)/shard_map/ppermute | solution.py:18
  426.3 63.7 %collective-permute-start.10 = (bf16[2,1056,16]{1,2,0:T(8,128)(2,1)S(1)}, bf16[2,1056,16]{1,2,0:T(8,128)(2,1)S(1)}, u32[]{:S(2)}, u32[]{:S(2)}) collective-permute-start(bf16[2,1056,16]{1,2,0:T(8,128)(2,1)S(1)} %copy.20), channel_id=1, source_target_pairs={{1,0},{2,1},{3,2},{4,3},{5,4},{6,5},{7,6},{9,8},{10,9},{11,10},{12... | collective-permute-start | bytes 202760 | tf_op jit(solution)/shard_map/ppermute | solution.py:20
  547.8 126.1 %copy-start.3 = (f32[1024,512]{1,0:T(8,128)S(1)}, f32[1024,512]{1,0:T(8,128)}, u32[]{:S(2)}) copy-start(f32[1024,512]{1,0:T(8,128)} %param.6) | copy-start | bytes 6291460
Sparse Core Ops, SparseCore 0:
  10.3 121.2 all-gather.11
  133.5 54.6 all-gather.9
  190.1 55.8 all-gather.13
  259.4 80.7 all-gather.17
  341.9 54.3 all-gather.15
  397.7 81.3 all-gather.25
  481.0 54.3 all-gather.23
  536.9 80.7 all-gather.19
  619.6 54.3 all-gather.21
